TPU v7x, 256 devices: a whole 4x4x8 slice. The times are simulated.
256 devices in a mesh: dp: 4 (over x), expert: 64 (over y, z, core).
Axes of the slice: x: 4, y: 4, z: 8, core: 2. Of those that a mesh axis runs over, the one named last changes fastest.
Arguments:
- hidden: bfloat16 [4, 4096, 2, 2048], P('dp', 'expert'), may hold values from -6 to 6
- queries: bfloat16 [4, 4096, 2, 4096], P('dp', 'expert'), may hold values from -45 to 45
- latents: bfloat16 [4, 4096, 2, 512], P('dp', 'expert'), may hold values from -165 to 165
- mem_latents: bfloat16 [4, 32, 2, 512], P('dp'), may hold values from -6 to 6
- lengths: int32 [4, 2], P('dp'), may hold values from 2048 to 4096
- ids: int32 [4, 4096, 2, 6], P('dp', 'expert'), may hold values from 0 to 63, all different within a row; in each aligned block of 128 rows (0 to 127, 128 to 255, ..., all dimensions but the last counted through in order) at most 14 rows name the same one
- gates: bfloat16 [4, 4096, 2, 6], P('dp', 'expert'), may hold values from 0.049804688 to 0.5
- norm_gain: bfloat16 [2048], replicated, may hold values from 0.25 to 1.75
- w_uv: bfloat16 [8, 512, 128], P('dp'), may hold values from -0.25 to 0.25
- w_out: bfloat16 [1024, 2048], P('dp'), may hold values from -0.1875 to 0.1875
- w_gate: bfloat16 [64, 2048, 704], P('expert'), may hold values from -0.125 to 0.125
- w_up: bfloat16 [64, 2048, 704], P('expert'), may hold values from -0.125 to 0.125
- w_down: bfloat16 [64, 704, 2048], P('expert'), may hold values from -0.21875 to 0.21875
Outputs:
- layer_out: bfloat16 [4, 4096, 2, 2048], P('dp', 'expert')
Inputs may be any that keep to these rules, and one draw needn't show every extreme that they name: `ids`: each row names 6 different experts; the rows of one device (aligned blocks of 128 rows in the order of the leading dimensions) name any one expert at most 14 times, a bound that some block reaches.
All inputs are finite; a program needn't handle non-finite values.
Results may differ from a plain program's by a relative error of at most 0.007.
Values may be sent and summed in bfloat16 or wider, within the bound.
A program may use at most 128 MiB of HBM per device.

v0:
```python
import jax
import jax.numpy as jnp
from jax import lax
from jax.sharding import PartitionSpec as P

score_scale = 192.0 ** (-0.5)
norm_eps = 1e-06


def sent_to_all(shard, axis):
    devices = lax.axis_size(axis)
    return lax.all_to_all(
        jnp.broadcast_to(shard[None], (devices, *shard.shape)), axis, 0, 0, tiled=True
    )


def joined_along(blocks, dim):
    dims = list(blocks.shape[1:])
    dims[dim] *= blocks.shape[0]
    return jnp.moveaxis(blocks, 0, dim).reshape(dims)


def gather_directly(shard, axis, dim):
    blocks = sent_to_all(shard, axis)
    return joined_along(blocks, dim)


def shards(
    hidden,
    queries,
    latents,
    mem_latents,
    lengths,
    ids,
    gates,
    norm_gain,
    w_uv,
    w_out,
    w_gate,
    w_up,
    w_down,
):
    local_len = hidden.shape[1]
    seq_count = hidden.shape[2]
    model_width = hidden.shape[3]
    latent_dim = latents.shape[3]
    head_count = queries.shape[3] // latent_dim
    row_count = local_len * seq_count
    owner_count = lax.axis_size("expert")
    shard_index = lax.axis_index("expert")
    own_pos = shard_index * local_len + jnp.arange(local_len, dtype=jnp.int32)
    query_rows = queries[0].reshape(local_len, seq_count, head_count, latent_dim)
    memory = mem_latents[0]
    seq_limit = lengths[0]
    mem_scores = (
        jnp.einsum("tshl,msl->shtm", query_rows, memory, preferred_element_type=jnp.float32)
        * score_scale
    )
    first_max = jnp.max(mem_scores, axis=3)
    mem_weights = jnp.exp(mem_scores - first_max[..., None])
    first_sum = jnp.sum(mem_weights, axis=3)
    first_acc = jnp.einsum(
        "shtm,msl->tshl",
        mem_weights.astype(jnp.bfloat16),
        memory,
        preferred_element_type=jnp.float32,
    )

    def fold_step(carry, portion):
        old_max, old_sum, old_acc = carry
        key_rows = portion[0]
        key_pos = jnp.arange(key_rows.shape[0], dtype=jnp.int32)
        scores = (
            jnp.einsum("tshl,jsl->shtj", query_rows, key_rows, preferred_element_type=jnp.float32)
            * score_scale
        )
        causal = key_pos[None, :] <= own_pos[:, None]
        inside = key_pos[None, :] < seq_limit[:, None]
        visible = causal[None, None, :, :] & inside[:, None, None, :]
        scores = jnp.where(visible, scores, -jnp.inf)
        new_max = jnp.maximum(old_max, jnp.max(scores, axis=3))
        weights = jnp.exp(scores - new_max[..., None])
        factor = jnp.exp(old_max - new_max)
        new_sum = old_sum * factor + jnp.sum(weights, axis=3)
        contrib = jnp.einsum(
            "shtj,jsl->tshl",
            weights.astype(jnp.bfloat16),
            key_rows,
            preferred_element_type=jnp.float32,
        )
        new_acc = old_acc * jnp.transpose(factor, (2, 0, 1))[..., None] + contrib
        return (new_max, new_sum, new_acc)

    portion = lax.all_gather(latents, "expert", axis=1, tiled=True)
    last_pos = jnp.max(own_pos)
    final_max, final_sum, final_acc = lax.cond(
        jnp.int32(0) <= last_pos,
        lambda state: fold_step(state, portion),
        lambda state: state,
        (first_max, first_sum, first_acc),
    )
    attended = (final_acc / jnp.transpose(final_sum, (2, 0, 1))[..., None]).astype(jnp.bfloat16)
    values = jnp.einsum(
        "tshl,hlv->tshv",
        attended,
        gather_directly(w_uv, "dp", 0),
        preferred_element_type=jnp.float32,
    ).astype(jnp.bfloat16)
    flat_values = values.reshape(row_count, -1)
    attn_out = jnp.dot(
        flat_values,
        lax.all_gather(w_out, "dp", axis=0, tiled=True),
        preferred_element_type=jnp.float32,
    )
    residual = hidden[0].reshape(row_count, model_width).astype(jnp.float32) + attn_out
    mean_square = jnp.mean(residual * residual, axis=-1, keepdims=True)
    normed = (residual * lax.rsqrt(mean_square + norm_eps) * norm_gain.astype(jnp.float32)).astype(
        jnp.bfloat16
    )
    experts_here = w_gate.shape[0]
    expert_count = owner_count * experts_here
    top_count = ids.shape[3]
    capacity = min(row_count, row_count * top_count // expert_count + 2)
    flat_ids = ids[0].reshape(row_count * top_count)
    onehot = (flat_ids[:, None] == jnp.arange(expert_count, dtype=jnp.int32)[None, :]).astype(
        jnp.int32
    )
    before = jnp.cumsum(onehot, axis=0) - onehot
    slot_within = jnp.sum(before * onehot, axis=1)
    slot_index = (flat_ids * capacity + slot_within).reshape(row_count, top_count)
    matching = (
        jnp.arange(expert_count * capacity, dtype=jnp.int32)[:, None, None]
        == slot_index[None, :, :]
    )
    placing = jnp.any(matching, axis=2).astype(jnp.bfloat16)
    gate_rows = gates[0].reshape(row_count, top_count).astype(jnp.float32)
    mixing = jnp.sum(jnp.where(matching, gate_rows[None, :, :], jnp.float32(0.0)), axis=2).astype(
        jnp.bfloat16
    )
    outgoing = jnp.dot(placing, normed, preferred_element_type=jnp.float32).astype(jnp.bfloat16)
    outgoing = outgoing.reshape(owner_count, experts_here, capacity, model_width)
    incoming = lax.all_to_all(outgoing, "expert", split_axis=0, concat_axis=0, tiled=True)
    gate_h = jnp.einsum("necd,edf->necf", incoming, w_gate, preferred_element_type=jnp.float32)
    up_h = jnp.einsum("necd,edf->necf", incoming, w_up, preferred_element_type=jnp.float32)
    act = (jax.nn.silu(gate_h) * up_h).astype(jnp.bfloat16)
    produced = jnp.einsum("necf,efd->necd", act, w_down, preferred_element_type=jnp.float32).astype(
        jnp.bfloat16
    )
    returned = lax.all_to_all(produced, "expert", split_axis=0, concat_axis=0, tiled=True)
    combined_rows = returned.reshape(expert_count * capacity, model_width)
    routed = jnp.einsum("st,sd->td", mixing, combined_rows, preferred_element_type=jnp.float32)
    layer_out = (residual + routed).astype(jnp.bfloat16)
    return layer_out.reshape(1, local_len, seq_count, model_width)


def solution(mesh):
    return jax.shard_map(
        shards,
        mesh=mesh,
        in_specs=(
            P("dp", "expert", None, None),
            P("dp", "expert", None, None),
            P("dp", "expert", None, None),
            P("dp", None, None, None),
            P("dp", None),
            P("dp", "expert", None, None),
            P("dp", "expert", None, None),
            P(),
            P("dp", None, None),
            P("dp", None),
            P("expert", None, None),
            P("expert", None, None),
            P("expert", None, None),
        ),
        out_specs=P("dp", "expert", None, None),
        check_vma=False,
    )
```

profile of v0, /device:TPU:1, one launch (start us, length us, event | category | flops | bytes accessed | tf_op | source)
XLA Modules:
  0.0 415.4 jit_solution(3627106416608245663)
XLA Ops:
  6.5 0.0 copy-start
  6.5 0.0 copy-start.4
  6.5 0.0 copy-start.3
  6.5 0.0 all-gather.3.cloned.1.call-start
  6.5 1.7 copy.55
  8.3 0.0 all-gather.3.cloned.1.call-update
  8.3 0.0 all-gather.5.cloned.1.call-start
  8.3 0.7 all-gather.5.cloned.1.call-update
  9.0 2.1 broadcast_in_dim.29
  11.1 4.8 %all-to-all-start = ((bf16[4,2,512,128]{3,2,1,0:T(8,128)(2,1)}), bf16[4,2,512,128]{3,2,1,0:T(8,128)(2,1)}, u32[]{:S(2)}, u32[]{:S(2)}) async-start(bf16[4,2,512,128]{3,2,1,0:T(8,128)(2,1)} %broadcast_in_dim.29), calls=%async_computation | async-start | bytes 2097152 | tf_op jit(solution)/shard_map/all_to_all | solution.py:12
  16.0 0.0 copy-start.5
  16.0 0.0 copy-done.4
  16.0 0.1 copy.60
  16.1 0.1 eq.43
  16.2 0.1 eq.39
  16.4 2.6 reshape.151
  19.0 0.7 fusion.68
  20.3 0.0 copy-done.3
  20.3 1.1 reshape.142
  21.5 1.8 reduce-window.6
  23.3 0.3 slice_reduce_fusion
  23.6 0.1 fusion.61
  23.7 0.1 reduce_sum.49
  23.9 2.5 fusion.69
  26.4 0.1 copy.59
  26.6 0.1 copy.63
  26.6 0.0 copy-done.5
  26.6 0.1 fusion.57
  26.7 2.7 convolution_bitcast_fusion
  29.4 0.4 fusion.33
  29.9 67.4 %all-gather.3.cloned.1.call-done = bf16[1,4096,2,512]{3,1,2,0:T(8,128)(2,1)} async-done(((bf16[1,64,2,512]{3,1,2,0:T(8,128)(2,1)}), bf16[1,4096,2,512]{3,1,2,0:T(8,128)(2,1)}) %all-gather.3.cloned.1.call-update) | async-done | bytes 8388624 | tf_op jit(solution)/shard_map/all_gather | solution.py:94
  97.3 38.6 %conditional.1 = ((f32[2,8,64]{2,1,0:T(8,128)S(1)}, f32[64,2,8,512]{3,0,2,1:T(8,128)})) conditional(s32[]{:T(128)} %convert_element_type.74, (f32[2,8,64]{2,1,0:T(8,128)S(1)}, f32[64,2,8,512]{3,0,2,1:T(8,128)}) %tuple.12, (s32[64]{0:T(128)S(1)}, s32[1,2]{1,0:T(1,128)}, bf16[1,4096,2,512]{3,1,2,0:T(8,128)(2,1)}, bf16[64,2,8,512]{3,2,1,0:T(8,128)(2,1)}, ...), branch_computations={%region_3.0_spmd, %region_4.7_spmd} | conditional | flops 8637918208 | bytes 75047200 | solution.py:96
  97.3 0.2 iota_compare_fusion
  97.5 0.7 iota_compare_fusion.1
  98.3 0.3 broadcast_and_fusion
  98.6 15.8 %fusion.2 = (f32[2,8,64]{2,1,0:T(8,128)}, f32[2,4096,64,8]{1,2,3,0:T(8,128)}) fusion(pred[2,64,4096]{2,1,0:T(8,128)(4,1)S(1)} %broadcast_and_fusion, bf16[64,2,8,512]{3,2,1,0:T(8,128)(2,1)} %get-tuple-element.57, bf16[1,4096,2,512]{3,1,2,0:T(8,128)(2,1)} %get-tuple-element.27), kind=kOutput, calls=%fused_computation.4 | convolution fusion | flops 4307549184 | bytes 26742784 | tf_op jit(solution)/shard_map/cond/branch_1_fun/tshl,jsl->shtj/dot_general | solution.py:74
  114.4 0.7 fusion.17
  115.1 12.4 %bitcast_add_fusion = f32[64,2,8,512]{3,0,2,1:T(8,128)} fusion(f32[64,2,8,512]{3,0,2,1:T(8,128)} %get-tuple-element.29, bf16[1,4096,2,512]{3,1,2,0:T(8,128)(2,1)} %get-tuple-element.27, f32[2,4096,64,8]{1,2,3,0:T(8,128)} %get-tuple-element.61, f32[2,8,64]{2,1,0:T(8,128)S(1)} %get-tuple-element.59, pred[2,64,4096]{2,1,0:T(8,128)(4,1)S(1)} %broadcast_and_fusion, ...), kind=kOutput, calls=%fused_computation.13 | convolution fusion | flops 4312793088 | bytes 29892608 | tf_op jit(solution)/shard_map/cond/branch_1_fun/shtj,jsl->tshl/dot_general | solution.py:85
  127.5 8.4 %fusion.1 = f32[2,8,64]{2,1,0:T(8,128)S(1)} fusion(f32[2,4096,64,8]{1,2,3,0:T(8,128)} %get-tuple-element.61, f32[2,8,64]{2,1,0:T(8,128)S(1)} %get-tuple-element.59, pred[2,64,4096]{2,1,0:T(8,128)(4,1)S(1)} %broadcast_and_fusion), kind=kLoop, calls=%fused_computation.3 | loop fusion | flops 16776192 | bytes 17309696 | tf_op jit(solution)/shard_map/cond/branch_1_fun/reduce_sum | solution.py:84
  135.9 0.0 all-to-all-done
  135.9 2.4 fusion.48
  138.3 0.2 copy.58
  138.5 7.6 %all-gather.5.cloned.1.call-done = bf16[1024,2048]{1,0:T(8,128)(2,1)} async-done(((bf16[256,2048]{1,0:T(8,128)(2,1)}), bf16[1024,2048]{1,0:T(8,128)(2,1)}) %all-gather.5.cloned.1.call-update) | async-done | bytes 4194320 | tf_op jit(solution)/shard_map/all_gather | solution.py:112
  146.1 3.3 multiply_reduce_fusion
  149.4 0.0 copy-start.1
  149.4 1.0 copy-done.1
  150.4 3.0 convolution_convert_fusion
  153.4 6.0 %reshape.134 = bf16[64,1,14,2048]{3,2,0,1:T(8,128)(2,1)} reshape(bf16[896,2048]{1,0:T(8,128)(2,1)} %convolution_convert_fusion) | data formatting | bytes 7340032 | tf_op jit(solution)/shard_map/reshape | solution.py:141
  159.4 107.3 %all_to_all.15 = bf16[64,1,14,2048]{3,2,1,0:T(8,128)(2,1)S(1)} all-to-all(bf16[64,1,14,2048]{3,2,1,0:T(8,128)(2,1)} %bitcast.151), channel_id=1, replica_groups=mesh['dp'=4,'expert'=64] {'expert'}, dimensions={0} | all-to-all | bytes 7340032 | tf_op jit(solution)/shard_map/all_to_all | solution.py:142
  266.7 1.9 copy-done.2
  268.6 0.0 copy-done.7
  268.6 8.7 %fusion.22 = f32[64,14,704]{2,0,1:T(8,128)} fusion(bf16[64,1,14,2048]{3,2,1,0:T(8,128)(2,1)S(1)} %all_to_all.15, bf16[1,2048,704]{1,2,0:T(8,128)(2,1)S(1)} %copy-done.7), kind=kOutput, calls=%fused_computation.25 | convolution fusion | flops 2583691264 | bytes 9076736 | tf_op jit(solution)/shard_map/necd,edf->necf/dot_general | solution.py:143
  277.3 0.0 copy-done
  277.3 12.9 %convert_bitcast_fusion = bf16[64,1,14,2048]{3,0,2,1:T(8,128)(2,1)} fusion(bf16[1,704,2048]{2,1,0:T(8,128)(2,1)S(1)} %copy-done, bf16[1,2048,704]{1,2,0:T(8,128)(2,1)} %param.26, bf16[64,1,14,2048]{3,2,1,0:T(8,128)(2,1)} %copy-done.2, f32[64,14,704]{2,0,1:T(8,128)} %fusion.22), kind=kOutput, calls=%fused_computation.27 | convolution fusion | flops 5173002240 | bytes 15630336 | tf_op jit(solution)/shard_map/necf,efd->necd/dot_general | solution.py:146
  290.2 6.0 %copy.68 = bf16[64,1,14,2048]{3,2,1,0:T(8,128)(2,1)} copy(bf16[64,1,14,2048]{3,0,2,1:T(8,128)(2,1)} %convert_bitcast_fusion) | data formatting | bytes 7340032 | tf_op jit(solution)/shard_map/convert_element_type | solution.py:146
  296.2 6.2 %all-to-all-start.2 = ((bf16[64,1,14,2048]{3,2,1,0:T(8,128)(2,1)}), bf16[64,1,14,2048]{3,2,1,0:T(8,128)(2,1)}, u32[]{:S(2)}, u32[]{:S(2)}) async-start(bf16[64,1,14,2048]{3,2,1,0:T(8,128)(2,1)} %copy.68), calls=%async_computation.2 | async-start | bytes 8388608 | tf_op jit(solution)/shard_map/all_to_all | solution.py:149
  302.4 0.0 copy-done.6
  302.4 0.1 copy.64
  302.6 0.1 copy.65
  302.6 1.0 select_reduce_fusion
  303.6 94.6 %all-to-all-done.2 = bf16[64,1,14,2048]{3,2,1,0:T(8,128)(2,1)} async-done(((bf16[64,1,14,2048]{3,2,1,0:T(8,128)(2,1)}), bf16[64,1,14,2048]{3,2,1,0:T(8,128)(2,1)}, u32[]{:S(2)}, u32[]{:S(2)}) %all-to-all-start.2) | async-done | bytes 3670048 | tf_op jit(solution)/shard_map/all_to_all | solution.py:149
  398.3 6.0 %reshape.140 = bf16[896,2048]{1,0:T(8,128)(2,1)} reshape(bf16[64,1,14,2048]{3,2,1,0:T(8,128)(2,1)} %all-to-all-done.2) | data formatting | bytes 7340032 | tf_op jit(solution)/shard_map/reshape | solution.py:150
  404.2 3.1 fusion.34
  407.4 1.1 reshape.141
  (11 shorter events, 0.1 us)
Async XLA Ops:
  6.5 270.8 %copy-start = (bf16[1,704,2048]{2,1,0:T(8,128)(2,1)S(1)}, bf16[1,704,2048]{2,1,0:T(8,128)(2,1)}, u32[]{:S(2)}) copy-start(bf16[1,704,2048]{2,1,0:T(8,128)(2,1)} %param.27) | copy-start | bytes 8650756
  6.5 9.4 %copy-start.4 = (s32[1,64,2,6]{1,2,3,0:T(2,128)S(1)}, s32[1,64,2,6]{1,2,3,0:T(2,128)}, u32[]{:S(2)}) copy-start(s32[1,64,2,6]{1,2,3,0:T(2,128)} %param.20) | copy-start | bytes 9220
  6.5 13.8 %copy-start.3 = (bf16[1,64,2,2048]{3,2,1,0:T(2,128)(2,1)S(1)}, bf16[1,64,2,2048]{3,2,1,0:T(2,128)(2,1)}, u32[]{:S(2)}) copy-start(bf16[1,64,2,2048]{3,2,1,0:T(2,128)(2,1)} %param.15) | copy-start | bytes 1572868
  6.5 90.8 %all-gather.3.cloned.1.call-start = ((), (), s32[]{:S(2)}) async-start(), calls=%async_computation.3 | async-start | bytes 8519680 | tf_op jit(solution)/shard_map/all_gather | solution.py:94
  8.3 137.8 %all-gather.5.cloned.1.call-start = ((), (), s32[]{:S(2)}) async-start(), calls=%async_computation.4 | async-start | bytes 5242880 | tf_op jit(solution)/shard_map/all_gather | solution.py:112
  11.1 124.8 %all-to-all-start = ((bf16[4,2,512,128]{3,2,1,0:T(8,128)(2,1)}), bf16[4,2,512,128]{3,2,1,0:T(8,128)(2,1)}, u32[]{:S(2)}, u32[]{:S(2)}) async-start(bf16[4,2,512,128]{3,2,1,0:T(8,128)(2,1)} %broadcast_in_dim.29), calls=%async_computation | async-start | bytes 2097152 | tf_op jit(solution)/shard_map/all_to_all | solution.py:12
  16.0 10.7 %copy-start.5 = (bf16[2048]{0:T(1024)(128)(2,1)S(1)}, bf16[2048]{0:T(1024)(128)(2,1)}, u32[]{:S(2)}) copy-start(bf16[2048]{0:T(1024)(128)(2,1)} %param.22) | copy-start | bytes 12292
  149.4 1.0 copy-start.1
  159.4 109.2 %copy-start.7 = (bf16[1,2048,704]{1,2,0:T(8,128)(2,1)S(1)}, bf16[1,2048,704]{1,2,0:T(8,128)(2,1)}, u32[]{:S(2)}) copy-start(bf16[1,2048,704]{1,2,0:T(8,128)(2,1)} %param.25) | copy-start | bytes 8650756
  266.7 1.9 copy-start.2
  296.2 6.2 %copy-start.6 = (bf16[1,64,2,6]{1,2,3,0:T(2,128)(2,1)S(1)}, bf16[1,64,2,6]{1,2,3,0:T(2,128)(2,1)}, u32[]{:S(2)}) copy-start(bf16[1,64,2,6]{1,2,3,0:T(2,128)(2,1)} %param.21) | copy-start | bytes 4612
  296.2 102.0 %all-to-all-start.2 = ((bf16[64,1,14,2048]{3,2,1,0:T(8,128)(2,1)}), bf16[64,1,14,2048]{3,2,1,0:T(8,128)(2,1)}, u32[]{:S(2)}, u32[]{:S(2)}) async-start(bf16[64,1,14,2048]{3,2,1,0:T(8,128)(2,1)} %copy.68), calls=%async_computation.2 | async-start | bytes 8388608 | tf_op jit(solution)/shard_map/all_to_all | solution.py:149
Sparse Core Ops, SparseCore 0:
  10.1 87.1 all-gather.2
  99.1 46.9 all-gather.4
where the time goes:
time: 416 us; the launch traced here: 415 us
  waiting for transfers between devices  170 us (41%)
  blocking collectives  107 us (26%)
  matrix products  66.9 us (16%)
  local copies, waits for them, and re-layouts  30.9 us (7%)
  other arithmetic  14.6 us (4%)
  between operations  14.2 us (3%)
  starting transfers between devices  11.1 us (3%)
    all_to_all x1, blocking collectives, shards(): lax.all_to_all(outgoing, 'expert', split_axis=0, concat_axis=0, tiled=True)  107 us
    all_to_all x1, waiting for transfers between devices, shards(): lax.all_to_all(produced, 'expert', split_axis=0, concat_axis=0, tiled=True)  94.6 us
    all_gather x1, waiting for transfers between devices, shards(): portion = lax.all_gather(latents, 'expert', axis=1, tiled=True)  67.4 us
    dot_general x1, matrix products, fold_step(): jnp.einsum('tshl,jsl->shtj', query_rows, key_rows, preferred_element_type...  15.8 us
    dot_general x1, matrix products, shards(): jnp.einsum('necf,efd->necd', act, w_down, preferred_element_type=jnp.floa...  12.9 us
    dot_general x1, matrix products, fold_step(): jnp.einsum('shtj,jsl->tshl', weights.astype(jnp.bfloat16), key_rows, pref...  12.4 us
    dot_general x1, matrix products, shards(): jnp.einsum('necd,edf->necf', incoming, w_gate, preferred_element_type=jnp...  8.67 us
    reduce_sum x1, other arithmetic, fold_step(): new_sum = old_sum * factor + jnp.sum(weights, axis=3)  8.39 us
  transfers between devices with their start and end apart: 4, of which 3 were waited for; matrix products, arithmetic and copies ran while one was open for 14% of the time, Pallas kernels for 0%

commit v1 on v0

--- a/solution.py
+++ b/solution.py
@@ -91,7 +91,9 @@
         new_acc = old_acc * jnp.transpose(factor, (2, 0, 1))[..., None] + contrib
         return (new_max, new_sum, new_acc)
 
-    portion = lax.all_gather(latents, "expert", axis=1, tiled=True)
+    portion = jnp.concatenate(
+        lax.all_to_all(jnp.stack([latents] * lax.axis_size("expert")), "expert", 0, 0), axis=1
+    )
     last_pos = jnp.max(own_pos)
     final_max, final_sum, final_acc = lax.cond(
         jnp.int32(0) <= last_pos,

time: 416 us -> 532 us (1.28)
  waiting for transfers between devices: 170 us -> 270 us
  starting transfers between devices: 11.1 us -> 23.9 us
  local copies, waits for them, and re-layouts: 30.9 us -> 43.6 us
  matrix products: 66.9 us -> 61.3 us
    all_to_all x0 -> x1, waiting for transfers between devices: none -> 175 us  [shards(): lax.all_to_all(jnp.stack([latents] * lax.axis_size('expert')), 'expert',...]
    all_gather x1 -> x0, waiting for transfers between devices: 67.4 us -> none  [shards(): portion = lax.all_gather(latents, 'expert', axis=1, tiled=True)]
    all_to_all x0 -> x1, starting transfers between devices: none -> 13.5 us  [shards(): lax.all_to_all(jnp.stack([latents] * lax.axis_size('expert')), 'expert',...]
    another operation x0 -> x3, local copies, waits for them, and re-layouts: none -> 13 us
    all_gather x1, waiting for transfers between devices: 7.61 us -> 0.02 us  [shards(): lax.all_gather(w_out, 'dp', axis=0, tiled=True)]
  transfers between devices with their start and end apart: 4 -> 4, of which waited for: 3 -> 2; matrix products, arithmetic and copies ran while one was open for 14% -> 11% of each run, Pallas kernels for 0% -> 0%
where the time goes in v1:
time: 532 us; the launch traced here: 531 us
  waiting for transfers between devices  270 us (51%)
  blocking collectives  102 us (19%)
  matrix products  61.3 us (12%)
  local copies, waits for them, and re-layouts  43.6 us (8%)
  starting transfers between devices  23.9 us (4%)
  other arithmetic  15.2 us (3%)
  between operations  14.3 us (3%)
    all_to_all x1, waiting for transfers between devices, shards(): lax.all_to_all(jnp.stack([latents] * lax.axis_size('expert')), 'expert',...  175 us
    all_to_all x1, blocking collectives, shards(): lax.all_to_all(outgoing, 'expert', split_axis=0, concat_axis=0, tiled=True)  102 us
    all_to_all x1, waiting for transfers between devices, shards(): lax.all_to_all(produced, 'expert', split_axis=0, concat_axis=0, tiled=True)  94.6 us
    dot_general x1, matrix products, fold_step(): jnp.einsum('tshl,jsl->shtj', query_rows, key_rows, preferred_element_type...  15.3 us
    all_to_all x1, starting transfers between devices, shards(): lax.all_to_all(jnp.stack([latents] * lax.axis_size('expert')), 'expert',...  13.5 us
    dot_general x1, matrix products, shards(): jnp.einsum('necf,efd->necd', act, w_down, preferred_element_type=jnp.floa...  12.9 us
  transfers between devices with their start and end apart: 4, of which 2 were waited for; matrix products, arithmetic and copies ran while one was open for 11% of the time, Pallas kernels for 0%

profile of v1, /device:TPU:1, one launch (start us, length us, event | category | flops | bytes accessed | tf_op | source)
XLA Modules:
  0.0 530.7 jit_solution(11339926104315359042)
XLA Ops:
  6.5 0.0 copy-start
  6.5 1.1 copy.56
  7.6 4.3 stack.2
  11.9 13.5 %all-to-all-start = ((bf16[64,1,64,2,512]{4,2,3,1,0:T(8,128)(2,1)}), bf16[64,1,64,2,512]{4,2,3,1,0:T(8,128)(2,1)}, u32[]{:S(2)}, u32[]{:S(2)}) async-start(bf16[64,1,64,2,512]{4,2,3,1,0:T(8,128)(2,1)} %stack.2), calls=%async_computation | async-start | bytes 16777216 | tf_op jit(solution)/shard_map/all_to_all | solution.py:95
  25.4 0.0 copy-start.6
  25.4 0.0 all-gather.2.cloned.1.call-start
  25.4 0.7 all-gather.2.cloned.1.call-update
  26.1 0.0 copy-done.8
  26.1 0.1 copy.62
  26.2 0.1 eq.43
  26.4 0.1 eq.39
  26.5 2.6 reshape.154
  29.1 0.6 fusion.64
  30.4 0.0 copy-done.6
  30.4 0.0 copy-start.9
  30.4 1.1 reshape.145
  31.6 1.8 reduce-window.6
  33.4 0.3 slice_reduce_fusion
  33.7 0.1 fusion.57
  33.8 0.1 reduce_sum.49
  34.0 2.5 fusion.65
  36.5 174.6 %all-to-all-done = bf16[64,1,64,2,512]{4,2,3,1,0:T(8,128)(2,1)} async-done(((bf16[64,1,64,2,512]{4,2,3,1,0:T(8,128)(2,1)}), bf16[64,1,64,2,512]{4,2,3,1,0:T(8,128)(2,1)}, u32[]{:S(2)}, u32[]{:S(2)}) %all-to-all-start) | async-done | bytes 8388640 | tf_op jit(solution)/shard_map/all_to_all | solution.py:95
  211.1 2.1 broadcast_in_dim.29
  213.2 4.2 all-to-all-start.1
  217.5 0.1 copy.61
  217.6 0.1 copy.65
  217.7 0.0 copy-done.9
  217.7 0.1 fusion.53
  217.8 0.0 copy-done.7
  217.8 1.8 convolution_bitcast_fusion
  219.6 0.4 fusion.29
  220.0 43.9 %conditional.1 = ((f32[2,8,64]{2,1,0:T(8,128)S(1)}, f32[64,2,8,512]{3,0,2,1:T(8,128)})) conditional(s32[]{:T(128)} %convert_element_type.74, (f32[2,8,64]{2,1,0:T(8,128)S(1)}, f32[64,2,8,512]{3,0,2,1:T(8,128)}) %tuple.12, (s32[64]{0:T(128)S(1)}, s32[1,2]{1,0:T(1,128)}, bf16[64,1,64,2,512]{4,2,3,1,0:T(8,128)(2,1)}, bf16[64,2,8,512]{3,2,1,0:T(8,128)(2,1)}, ...), branch_computations={%region_3.0_spmd, %region_4.7_spmd} | conditional | flops 8637918208 | bytes 142156160 | solution.py:98
  220.2 0.2 iota_compare_fusion
  220.4 0.7 iota_compare_fusion.1
  221.2 0.3 broadcast_and_fusion
  221.5 7.7 %copy.57 = bf16[64,1,64,2,512]{4,2,0,3,1:T(8,128)(2,1)} copy(bf16[64,1,64,2,512]{4,2,3,1,0:T(8,128)(2,1)} %get-tuple-element.52) | data formatting | bytes 16777216 | tf_op jit(solution)/shard_map
  229.2 15.3 %fusion.2 = (f32[2,8,64]{2,1,0:T(8,128)}, f32[2,4096,64,8]{1,2,3,0:T(8,128)}) fusion(pred[2,64,4096]{2,1,0:T(8,128)(4,1)S(1)} %broadcast_and_fusion, bf16[4096,2,512,1]{2,0,3,1:T(8,128)(2,1)} %bitcast.148, bf16[64,2,8,512]{3,2,1,0:T(8,128)(2,1)} %get-tuple-element.57), kind=kOutput, calls=%fused_computation.4 | convolution fusion | flops 4307549184 | bytes 26742784 | tf_op jit(solution)/shard_map/cond/branch_1_fun/tshl,jsl->shtj/dot_general | solution.py:74
  244.5 0.7 fusion.13
  245.3 9.1 %fusion.1 = f32[2,8,64]{2,1,0:T(8,128)S(1)} fusion(f32[2,4096,64,8]{1,2,3,0:T(8,128)} %get-tuple-element.61, f32[2,8,64]{2,1,0:T(8,128)S(1)} %get-tuple-element.59, pred[2,64,4096]{2,1,0:T(8,128)(4,1)S(1)} %broadcast_and_fusion), kind=kLoop, calls=%fused_computation.3 | loop fusion | flops 16776192 | bytes 17309696 | tf_op jit(solution)/shard_map/cond/branch_1_fun/reduce_sum | solution.py:84
  254.3 0.0 copy-done.2
  254.4 0.0 copy-done.4
  254.4 8.3 %bitcast_add_fusion = f32[64,2,8,512]{3,0,2,1:T(8,128)S(1)} fusion(f32[64,2,8,512]{3,0,2,1:T(8,128)S(1)} %copy-done.4, bf16[4096,2,512,1]{2,0,3,1:T(8,128)(2,1)S(1)} %bitcast.149, f32[2,4096,64,8]{1,2,3,0:T(8,128)} %get-tuple-element.61, f32[2,8,64]{2,1,0:T(8,128)S(1)} %get-tuple-element.59, pred[2,64,4096]{2,1,0:T(8,128)(4,1)S(1)} %broadcast_and_fusion, ...), kind=kOutput, calls=%fused_computation.10 | convolution fusion | flops 4312793088 | bytes 29892608 | tf_op jit(solution)/shard_map/cond/branch_1_fun/shtj,jsl->tshl/dot_general | solution.py:85
  262.7 1.3 copy-done.5
  264.0 0.0 all-to-all-done.1
  264.0 2.4 fusion.44
  266.3 0.2 copy.60
  266.5 0.0 all-gather.2.cloned.1.call-done
  266.5 3.3 multiply_reduce_fusion
  269.9 1.0 copy-done.1
  270.8 3.0 convolution_convert_fusion
  273.9 6.0 %reshape.137 = bf16[64,1,14,2048]{3,2,0,1:T(8,128)(2,1)} reshape(bf16[896,2048]{1,0:T(8,128)(2,1)} %convolution_convert_fusion) | data formatting | bytes 7340032 | tf_op jit(solution)/shard_map/reshape | solution.py:143
  279.9 102.2 %all_to_all.20 = bf16[64,1,14,2048]{3,2,1,0:T(8,128)(2,1)S(1)} all-to-all(bf16[64,1,14,2048]{3,2,1,0:T(8,128)(2,1)} %bitcast.147), channel_id=1, replica_groups=mesh['dp'=4,'expert'=64] {'expert'}, dimensions={0} | all-to-all | bytes 7340032 | tf_op jit(solution)/shard_map/all_to_all | solution.py:144
  382.1 1.9 copy-done.3
  384.0 8.7 %fusion.18 = f32[64,14,704]{2,0,1:T(8,128)} fusion(bf16[64,1,14,2048]{3,2,1,0:T(8,128)(2,1)S(1)} %all_to_all.20, bf16[1,2048,704]{1,2,0:T(8,128)(2,1)S(1)} %copy-done.11), kind=kOutput, calls=%fused_computation.23 | convolution fusion | flops 2583691264 | bytes 9076736 | tf_op jit(solution)/shard_map/necd,edf->necf/dot_general | solution.py:145
  392.7 12.9 %convert_bitcast_fusion = bf16[64,1,14,2048]{3,0,2,1:T(8,128)(2,1)} fusion(bf16[1,704,2048]{2,1,0:T(8,128)(2,1)S(1)} %copy-done, bf16[1,2048,704]{1,2,0:T(8,128)(2,1)} %param.26, bf16[64,1,14,2048]{3,2,1,0:T(8,128)(2,1)} %copy-done.3, f32[64,14,704]{2,0,1:T(8,128)} %fusion.18), kind=kOutput, calls=%fused_computation.25 | convolution fusion | flops 5173002240 | bytes 15630336 | tf_op jit(solution)/shard_map/necf,efd->necd/dot_general | solution.py:148
  405.6 6.0 %copy.70 = bf16[64,1,14,2048]{3,2,1,0:T(8,128)(2,1)} copy(bf16[64,1,14,2048]{3,0,2,1:T(8,128)(2,1)} %convert_bitcast_fusion) | data formatting | bytes 7340032 | tf_op jit(solution)/shard_map/convert_element_type | solution.py:148
  411.6 6.2 %all-to-all-start.3 = ((bf16[64,1,14,2048]{3,2,1,0:T(8,128)(2,1)}), bf16[64,1,14,2048]{3,2,1,0:T(8,128)(2,1)}, u32[]{:S(2)}, u32[]{:S(2)}) async-start(bf16[64,1,14,2048]{3,2,1,0:T(8,128)(2,1)} %copy.70), calls=%async_computation.3 | async-start | bytes 8388608 | tf_op jit(solution)/shard_map/all_to_all | solution.py:151
  417.8 0.1 copy.66
  417.9 0.1 copy.67
  418.0 1.0 select_reduce_fusion
  419.0 94.6 %all-to-all-done.3 = bf16[64,1,14,2048]{3,2,1,0:T(8,128)(2,1)} async-done(((bf16[64,1,14,2048]{3,2,1,0:T(8,128)(2,1)}), bf16[64,1,14,2048]{3,2,1,0:T(8,128)(2,1)}, u32[]{:S(2)}, u32[]{:S(2)}) %all-to-all-start.3) | async-done | bytes 3670048 | tf_op jit(solution)/shard_map/all_to_all | solution.py:151
  513.7 6.0 %reshape.143 = bf16[896,2048]{1,0:T(8,128)(2,1)} reshape(bf16[64,1,14,2048]{3,2,1,0:T(8,128)(2,1)} %all-to-all-done.3) | data formatting | bytes 7340032 | tf_op jit(solution)/shard_map/reshape | solution.py:152
  519.6 3.1 fusion.30
  522.8 1.1 reshape.144
  (20 shorter events, 0.1 us)
Async XLA Ops:
  6.5 386.1 %copy-start = (bf16[1,704,2048]{2,1,0:T(8,128)(2,1)S(1)}, bf16[1,704,2048]{2,1,0:T(8,128)(2,1)}, u32[]{:S(2)}) copy-start(bf16[1,704,2048]{2,1,0:T(8,128)(2,1)} %param.27) | copy-start | bytes 8650756
  11.9 14.2 %copy-start.8 = (s32[1,64,2,6]{1,2,3,0:T(2,128)S(1)}, s32[1,64,2,6]{1,2,3,0:T(2,128)}, u32[]{:S(2)}) copy-start(s32[1,64,2,6]{1,2,3,0:T(2,128)} %param.20) | copy-start | bytes 9220
  11.9 199.2 %all-to-all-start = ((bf16[64,1,64,2,512]{4,2,3,1,0:T(8,128)(2,1)}), bf16[64,1,64,2,512]{4,2,3,1,0:T(8,128)(2,1)}, u32[]{:S(2)}, u32[]{:S(2)}) async-start(bf16[64,1,64,2,512]{4,2,3,1,0:T(8,128)(2,1)} %stack.2), calls=%async_computation | async-start | bytes 16777216 | tf_op jit(solution)/shard_map/all_to_all | solution.py:95
  25.4 5.1 copy-start.6
  25.4 241.2 %all-gather.2.cloned.1.call-start = ((), (), s32[]{:S(2)}) async-start(), calls=%async_computation.4 | async-start | bytes 5242880 | tf_op jit(solution)/shard_map/all_gather | solution.py:114
  30.4 187.3 %copy-start.9 = (bf16[2048]{0:T(1024)(128)(2,1)S(1)}, bf16[2048]{0:T(1024)(128)(2,1)}, u32[]{:S(2)}) copy-start(bf16[2048]{0:T(1024)(128)(2,1)} %param.22) | copy-start | bytes 12292
  31.6 186.2 %copy-start.7 = (bf16[1,32,2,512]{3,2,1,0:T(2,128)(2,1)S(1)}, bf16[1,32,2,512]{3,2,1,0:T(2,128)(2,1)}, u32[]{:S(2)}) copy-start(bf16[1,32,2,512]{3,2,1,0:T(2,128)(2,1)} %param.18) | copy-start | bytes 196612
  213.2 50.8 %all-to-all-start.1 = ((bf16[4,2,512,128]{3,2,1,0:T(8,128)(2,1)}), bf16[4,2,512,128]{3,2,1,0:T(8,128)(2,1)}, u32[]{:S(2)}, u32[]{:S(2)}) async-start(bf16[4,2,512,128]{3,2,1,0:T(8,128)(2,1)} %broadcast_in_dim.29), calls=%async_computation.1 | async-start | bytes 2097152 | tf_op jit(solution)/shard_map/all_to_all | solution.py:12
  245.2 9.1 %copy-start.2 = (bf16[64,1,64,2,512]{4,2,0,3,1:T(8,128)(2,1)S(1)}, bf16[64,1,64,2,512]{4,2,0,3,1:T(8,128)(2,1)}, u32[]{:S(2)}) copy-start(bf16[64,1,64,2,512]{4,2,0,3,1:T(8,128)(2,1)} %copy.57) | copy-start | bytes 25165828 | tf_op jit(solution)/shard_map/cond
  245.2 9.1 %copy-start.4 = (f32[64,2,8,512]{3,0,2,1:T(8,128)S(1)}, f32[64,2,8,512]{3,0,2,1:T(8,128)}, u32[]{:S(2)}) copy-start(f32[64,2,8,512]{3,0,2,1:T(8,128)} %get-tuple-element.29) | copy-start | bytes 6291460 | tf_op jit(solution)/shard_map/cond
  262.7 1.3 copy-start.5
  269.8 1.0 copy-start.1
  279.9 104.1 %copy-start.11 = (bf16[1,2048,704]{1,2,0:T(8,128)(2,1)S(1)}, bf16[1,2048,704]{1,2,0:T(8,128)(2,1)}, u32[]{:S(2)}) copy-start(bf16[1,2048,704]{1,2,0:T(8,128)(2,1)} %param.25) | copy-start | bytes 8650756
  382.1 1.9 copy-start.3
  411.6 6.2 %copy-start.10 = (bf16[1,64,2,6]{1,2,3,0:T(2,128)(2,1)S(1)}, bf16[1,64,2,6]{1,2,3,0:T(2,128)(2,1)}, u32[]{:S(2)}) copy-start(bf16[1,64,2,6]{1,2,3,0:T(2,128)(2,1)} %param.21) | copy-start | bytes 4612
  411.6 102.0 %all-to-all-start.3 = ((bf16[64,1,14,2048]{3,2,1,0:T(8,128)(2,1)}), bf16[64,1,14,2048]{3,2,1,0:T(8,128)(2,1)}, u32[]{:S(2)}, u32[]{:S(2)}) async-start(bf16[64,1,14,2048]{3,2,1,0:T(8,128)(2,1)} %copy.70), calls=%async_computation.3 | async-start | bytes 8388608 | tf_op jit(solution)/shard_map/all_to_all | solution.py:151
Sparse Core Ops, SparseCore 0:
  28.0 51.5 all-gather.1
